TPU v7x, 256 devices: a 4x2x16 block of a 4x16x16 slice. The times are simulated.
256 devices in a mesh: grp: 2 (over y), row: 32 (over z, core), col: 4 (over x).
Axes of the slice: x: 4, y: 2, z: 16, core: 2. Of those that a mesh axis runs over, the one named last changes fastest.
The devices are a block of a 4x16x16 slice.
Arguments:
- pair: bfloat16 [768, 384, 128], P(('grp', 'row'), 'col'), parts along dimension 0, may hold values from -6 to 6
- token_count: int32 [2], P('grp'), parts along dimension 0, may hold values from 288 to 384
- tri_in: bfloat16 [2, 128, 512], replicated, may hold values from -0.5 to 0.5
- tri_gate: bfloat16 [2, 128, 128], replicated, may hold values from -0.5 to 0.5
- tri_out: bfloat16 [2, 128, 128], replicated, may hold values from -0.5 to 0.5
- trans_in: bfloat16 [128, 1024], replicated, may hold values from -0.5 to 0.5
- trans_out: bfloat16 [512, 128], replicated, may hold values from -0.25 to 0.25
Outputs:
- pair_out: bfloat16 [768, 384, 128], P(('grp', 'row'), 'col'), parts along dimension 0
There are 2 independent parts, one for each index of `grp`. A program takes and returns all parts, laid end to end along the dimension named above; an argument that names none is the same for every part. Nothing has to cross between parts.
Inputs may be any that keep to these rules, and one draw needn't show every extreme that they name: `token_count`: the number of real tokens of the complex; pair entries with either token index at or past it are padding.
All inputs are finite; a program needn't handle non-finite values.
Results may differ from a plain program's by a relative error of at most 0.015.
Values may be sent and summed in bfloat16 or wider, within the bound.
A program may use at most 64 MiB of HBM per device.

v0:
```python
import jax
import jax.numpy as jnp
from jax import lax
from jax.sharding import Mesh
from jax.sharding import PartitionSpec as P

ROW = ("row_0", "row_1")
GRP_ROW = ("grp", "row_0", "row_1")


def split_up(value, dim, size):
    lengths = value.shape
    blocks = value.reshape(*lengths[:dim], size, lengths[dim] // size, *lengths[dim + 1 :])
    return jnp.moveaxis(blocks, dim, 0)


def sum_at_owner(value, axis, dim):
    blocks = split_up(value, dim, lax.axis_size(axis))
    arrived = lax.all_to_all(blocks, axis, split_axis=0, concat_axis=0, tiled=True)
    return arrived.sum(axis=0)


def sent_to_all(value, axis):
    copies = jnp.broadcast_to(value, (lax.axis_size(axis), *value.shape))
    return lax.all_to_all(copies, axis, split_axis=0, concat_axis=0, tiled=True)


def laid_out(blocks, dim):
    lengths = list(blocks.shape[1:])
    lengths[dim] *= blocks.shape[0]
    return jnp.moveaxis(blocks, 0, dim).reshape(lengths)


def gather_directly(value, axis, dim):
    blocks = sent_to_all(value, axis)
    return laid_out(blocks, dim)


def exchange_in_order(blocks, axes, sequence):
    lengths = [lax.axis_size(a) for a in axes]
    blocks = blocks.reshape(*lengths, *blocks.shape[1:])
    for k in sequence:
        blocks = lax.all_to_all(blocks, axes[k], split_axis=k, concat_axis=k, tiled=True)
    return blocks.reshape(-1, *blocks.shape[len(axes) :])


def two_step_exchange(value, groups, sequence, split_dim, concat_dim):
    size = lax.axis_size(groups[0]) * lax.axis_size(groups[1])
    blocks = split_up(value, split_dim, size)
    return laid_out(exchange_in_order(blocks, groups, sequence), concat_dim)


def layer_norm(values, along):
    average = jnp.mean(values, axis=along, keepdims=True)
    centred = values - average
    spread = jnp.mean(centred * centred, axis=along, keepdims=True)
    return centred * lax.rsqrt(spread + 1e-05)


def contract_rows(left_side, right_side):
    return jnp.einsum("hik,hjk->hij", left_side, right_side, preferred_element_type=jnp.float32)


def contract_columns(left_side, right_side):
    return jnp.einsum("hki,hkj->hij", left_side, right_side, preferred_element_type=jnp.float32)


def body(pair, token_count, tri_in, tri_gate, tri_out, trans_in, trans_out):
    tile_rows, tile_cols, pair_width = pair.shape
    hidden = tri_out.shape[1]
    ffn_width = trans_out.shape[0]
    row_place = lax.axis_index(ROW)
    col_place = lax.axis_index("col")
    row_first = row_place * tile_rows
    col_first = col_place * tile_cols
    token_limit = token_count[0]
    row_keep = (row_first + jnp.arange(tile_rows, dtype=jnp.int32) < token_limit).astype(
        jnp.float32
    )
    col_keep = (col_first + jnp.arange(tile_cols, dtype=jnp.int32) < token_limit).astype(
        jnp.float32
    )
    keep_mask = row_keep[:, None] * col_keep[None, :]

    def project(stream, which_side):
        normed = layer_norm(stream.astype(jnp.float32), 2).astype(jnp.bfloat16)
        weight = tri_in[which_side].reshape(pair_width, 4, hidden)
        projected = jnp.einsum("ijc,cgh->ghij", normed, weight, preferred_element_type=jnp.float32)
        left_side = (keep_mask * jax.nn.sigmoid(projected[2]) * projected[0]).astype(jnp.bfloat16)
        right_side = (keep_mask * jax.nn.sigmoid(projected[3]) * projected[1]).astype(jnp.bfloat16)
        gate_value = jax.nn.sigmoid(
            jnp.dot(normed, tri_gate[which_side], preferred_element_type=jnp.float32)
        )
        return (left_side, right_side, gate_value)

    def finish(stream, mixed_sum, gate_value, which_side):
        normed = layer_norm(mixed_sum, 0).astype(jnp.bfloat16)
        update = gate_value * jnp.einsum(
            "hij,hc->ijc", normed, tri_out[which_side], preferred_element_type=jnp.float32
        )
        return (stream.astype(jnp.float32) + keep_mask[:, :, None] * update).astype(jnp.bfloat16)

    left_side, right_side, gate_value = project(pair, 0)
    partial_rows = contract_rows(left_side, lax.all_gather(right_side, ROW, axis=1, tiled=True))
    mixed_sum = sum_at_owner(partial_rows, "col", 2)
    stream = finish(pair, mixed_sum, gate_value, 0)
    left_side, right_side, gate_value = project(stream, 1)
    left_rows = gather_directly(left_side, "col", 2)
    column_strip = two_step_exchange(left_rows, ("row_0", "row_1"), (1, 0), 2, 1)
    mixed_sum = contract_columns(column_strip, lax.all_gather(right_side, ROW, axis=1, tiled=True))
    stream = finish(stream, mixed_sum, gate_value, 1)
    normed = layer_norm(stream.astype(jnp.float32), 2).astype(jnp.bfloat16)
    inner_sum = jnp.dot(normed, trans_in, preferred_element_type=jnp.float32)
    activation = (jax.nn.silu(inner_sum[..., :ffn_width]) * inner_sum[..., ffn_width:]).astype(
        jnp.bfloat16
    )
    update = jnp.dot(activation, trans_out, preferred_element_type=jnp.float32)
    return (stream.astype(jnp.float32) + keep_mask[:, :, None] * update).astype(jnp.bfloat16)


def solution(mesh):
    torus = Mesh(
        mesh.devices.reshape(mesh.shape["grp"], 16, 2, mesh.shape["col"]),
        ("grp", "row_0", "row_1", "col"),
    )
    placed = (P(GRP_ROW, "col", None), P("grp"), P(), P(), P(), P(), P())
    return jax.shard_map(
        body, mesh=torus, in_specs=placed, out_specs=P(GRP_ROW, "col", None), check_vma=False
    )
```

profile of v0, /device:TPU:33, one launch (start us, length us, event | category | flops | bytes accessed | tf_op | source)
XLA Modules:
  0.0 327.6 jit_solution(5073324090975161739)
XLA Ops:
  7.2 1.1 convert_reduce_fusion
  8.4 1.4 fusion.20
  9.9 1.0 fusion.74
  11.1 1.5 convolution_bitcast_fusion.1
  12.6 1.1 fusion.37
  13.7 1.2 copy.55
  14.9 91.9 %all-gather.3.cloned.1.call-done = bf16[128,384,96]{0,2,1:T(8,128)(2,1)} async-done(((bf16[128,12,96]{0,2,1:T(8,128)(2,1)}), bf16[128,384,96]{0,2,1:T(8,128)(2,1)}) %all-gather.3.cloned.1.call-update) | async-done | bytes 9437200 | tf_op jit(solution)/shard_map/all_gather | solution.py:104
  106.8 15.6 %copy.56 = bf16[128,384,96]{2,1,0:T(8,128)(2,1)} copy(bf16[128,384,96]{0,2,1:T(8,128)(2,1)} %all-gather.3.cloned.1.call-done) | data formatting | bytes 18874368 | tf_op jit(solution)/shard_map/all_gather | solution.py:104
  122.4 9.2 %fusion.78 = f32[128,12,384]{2,1,0:T(8,128)S(1)} fusion(bf16[128,12,96]{2,1,0:T(8,128)(2,1)} %copy.55, bf16[128,384,96]{2,1,0:T(8,128)(2,1)} %copy.56), kind=kOutput, calls=%fused_computation.114 | convolution fusion | flops 113246208 | bytes 12091392 | tf_op jit(solution)/shard_map/hik,hjk->hij/dot_general | solution.py:61
  131.6 2.1 copy.57
  133.7 3.3 copy.58
  136.9 4.1 %all-to-all-start = ((f32[4,128,12,96]{1,3,2,0:T(8,128)}), f32[4,128,12,96]{1,3,2,0:T(8,128)S(1)}, u32[]{:S(2)}, u32[]{:S(2)}) async-start(f32[4,128,12,96]{1,3,2,0:T(8,128)} %copy.58), calls=%async_computation | async-start | bytes 4718592 | tf_op jit(solution)/shard_map/all_to_all | solution.py:19
  141.1 0.8 copy.81
  141.8 1.3 fusion.11
  143.1 26.6 %all-to-all-done = f32[4,128,12,96]{1,3,2,0:T(8,128)S(1)} async-done(((f32[4,128,12,96]{1,3,2,0:T(8,128)}), f32[4,128,12,96]{1,3,2,0:T(8,128)S(1)}, u32[]{:S(2)}, u32[]{:S(2)}) %all-to-all-start) | async-done | bytes 2359328 | tf_op jit(solution)/shard_map/all_to_all | solution.py:19
  172.4 1.1 fusion.23
  173.7 17.4 %all_to_all.20 = bf16[4,128,12,96]{1,3,2,0:T(8,128)(2,1)S(1)} all-to-all(bf16[4,128,12,96]{1,3,2,0:T(8,128)(2,1)S(1)} %broadcast_in_dim.2), channel_id=1, replica_groups=mesh['grp'=2,'row_0'=16,'row_1'=2,'col'=4] {'col'}, dimensions={0} | all-to-all | bytes 2359296 | tf_op jit(solution)/shard_map/all_to_all | solution.py:25
  191.0 1.1 copy.62
  192.1 2.2 reshape_reshape.3
  194.8 7.1 %all_to_all.21 = bf16[16,2,128,12,12]{2,0,4,3,1:T(8,128)(2,1)S(1)} all-to-all(bf16[16,2,128,12,12]{2,0,4,3,1:T(8,128)(2,1)S(1)} %copy.63), channel_id=1, replica_groups=mesh['grp'=2,'row_0'=16,'row_1'=2,'col'=4] {'row_1'}, dimensions={1} | all-to-all | bytes 2359296 | tf_op jit(solution)/shard_map/all_to_all | solution.py:43
  201.9 2.2 copy.64
  204.1 6.6 %all-to-all-start.3 = ((bf16[16,2,128,12,12]{2,1,4,3,0:T(2,128)(2,1)}), bf16[16,2,128,12,12]{2,1,4,3,0:T(2,128)(2,1)S(1)}, u32[]{:S(2)}, u32[]{:S(2)}) async-start(bf16[16,2,128,12,12]{2,1,4,3,0:T(2,128)(2,1)} %copy.64), calls=%async_computation.3 | async-start | bytes 2359296 | tf_op jit(solution)/shard_map/all_to_all | solution.py:43
  211.2 66.2 %all-to-all-done.3 = bf16[16,2,128,12,12]{2,1,4,3,0:T(2,128)(2,1)S(1)} async-done(((bf16[16,2,128,12,12]{2,1,4,3,0:T(2,128)(2,1)}), bf16[16,2,128,12,12]{2,1,4,3,0:T(2,128)(2,1)S(1)}, u32[]{:S(2)}, u32[]{:S(2)}) %all-to-all-start.3) | async-done | bytes 1179680 | tf_op jit(solution)/shard_map/all_to_all | solution.py:43
  277.4 1.0 copy.65
  278.5 0.8 copy.66
  279.3 1.2 reshape.165
  280.4 2.2 copy.67
  282.6 12.4 %all-gather.5.cloned.1.call-done = bf16[128,384,96]{0,2,1:T(8,128)(2,1)} async-done(((bf16[128,12,96]{0,2,1:T(8,128)(2,1)}), bf16[128,384,96]{0,2,1:T(8,128)(2,1)}) %all-gather.5.cloned.1.call-update) | async-done | bytes 9437200 | tf_op jit(solution)/shard_map/all_gather | solution.py:110
  295.0 15.6 %copy.68 = bf16[128,384,96]{2,1,0:T(8,128)(2,1)} copy(bf16[128,384,96]{0,2,1:T(8,128)(2,1)} %all-gather.5.cloned.1.call-done) | data formatting | bytes 18874368 | tf_op jit(solution)/shard_map/all_gather | solution.py:110
  310.6 5.8 %fusion.76 = (f32[12,96]{1,0:T(8,128)S(1)}, f32[128,12,96]{2,1,0:T(8,128)S(1)}) fusion(bf16[128,384,12]{1,2,0:T(8,128)(2,1)S(1)} %copy.67, bf16[128,384,96]{2,1,0:T(8,128)(2,1)} %copy.68), kind=kOutput, calls=%fused_computation.112 | convolution fusion | flops 113392512 | bytes 11211264 | tf_op jit(solution)/shard_map/hki,hkj->hij/dot_general | solution.py:65
  318.4 0.8 fusion.53
  319.3 1.5 fusion.16
  (46 shorter events, 6.0 us)
Async XLA Ops:
  6.5 311.8 %copy-start = (bf16[128,1024]{1,0:T(8,128)(2,1)S(1)}, bf16[128,1024]{1,0:T(8,128)(2,1)}, u32[]{:S(2)}) copy-start(bf16[128,1024]{1,0:T(8,128)(2,1)} %param.12) | copy-start | bytes 786436
  6.6 100.3 %all-gather.3.cloned.1.call-start = ((), (), s32[]{:S(2)}) async-start(), calls=%async_computation.4 | async-start | bytes 9732096 | tf_op jit(solution)/shard_map/all_gather | solution.py:104
  9.9 1.2 copy-start.5
  136.9 4.9 %copy-start.1 = (bf16[12,96,128]{2,1,0:T(8,128)(2,1)S(1)}, bf16[12,96,128]{2,1,0:T(8,128)(2,1)}, u32[]{:S(2)}) copy-start(bf16[12,96,128]{2,1,0:T(8,128)(2,1)} %param.7) | copy-start | bytes 884740
  136.9 32.8 %all-to-all-start = ((f32[4,128,12,96]{1,3,2,0:T(8,128)}), f32[4,128,12,96]{1,3,2,0:T(8,128)S(1)}, u32[]{:S(2)}, u32[]{:S(2)}) async-start(f32[4,128,12,96]{1,3,2,0:T(8,128)} %copy.58), calls=%async_computation | async-start | bytes 4718592 | tf_op jit(solution)/shard_map/all_to_all | solution.py:19
  141.1 153.9 %all-gather.5.cloned.1.call-start = ((), (), s32[]{:S(2)}) async-start(), calls=%async_computation.5 | async-start | bytes 9732096 | tf_op jit(solution)/shard_map/all_gather | solution.py:110
  169.7 0.8 copy-start.3
  170.0 1.8 copy-start.2
  201.9 8.8 %copy-start.7 = (bf16[2,128,128]{2,1,0:T(8,128)(2,1)S(1)}, bf16[2,128,128]{2,1,0:T(8,128)(2,1)}, u32[]{:S(2)}) copy-start(bf16[2,128,128]{2,1,0:T(8,128)(2,1)} %param.10) | copy-start | bytes 196612
  204.1 73.3 %all-to-all-start.3 = ((bf16[16,2,128,12,12]{2,1,4,3,0:T(2,128)(2,1)}), bf16[16,2,128,12,12]{2,1,4,3,0:T(2,128)(2,1)S(1)}, u32[]{:S(2)}, u32[]{:S(2)}) async-start(bf16[16,2,128,12,12]{2,1,4,3,0:T(2,128)(2,1)} %copy.64), calls=%async_computation.3 | async-start | bytes 2359296 | tf_op jit(solution)/shard_map/all_to_all | solution.py:43
  316.4 0.8 copy-start.4
  318.4 0.9 copy-start.6
Sparse Core Ops, SparseCore 0:
  13.8 92.9 all-gather.2
  173.6 121.3 all-gather.4
where the time goes:
time: 329 us; the launch traced here: 328 us
  waiting for transfers between devices  197 us (60%)
  local copies, waits for them, and re-layouts  51.5 us (16%)
  blocking collectives  24.4 us (7%)
  matrix products  22.5 us (7%)
  between operations  14.4 us (4%)
  starting transfers between devices  10.7 us (3%)
  other arithmetic  6.82 us (2%)
    all_gather x2, waiting for transfers between devices, body(): lax.all_gather(right_side, ROW, axis=1, tiled=True)  104 us
    all_to_all x1, waiting for transfers between devices, exchange_in_order(): lax.all_to_all(blocks, axes[k], split_axis=k, concat_axis=k, tiled=True)  66.2 us
    all_gather x2, local copies, waits for them, and re-layouts, body(): lax.all_gather(right_side, ROW, axis=1, tiled=True)  31.1 us
    all_to_all x1, waiting for transfers between devices, sum_at_owner(): lax.all_to_all(blocks, axis, split_axis=0, concat_axis=0, tiled=True)  26.6 us
    all_to_all x1, blocking collectives, sent_to_all(): return lax.all_to_all(copies, axis, split_axis=0, concat_axis=0, tiled=True)  17.4 us
    dot_general x1, matrix products, contract_rows(): jnp.einsum('hik,hjk->hij', left_side, right_side, preferred_element_type=...  9.19 us
    all_to_all x1, blocking collectives, exchange_in_order(): lax.all_to_all(blocks, axes[k], split_axis=k, concat_axis=k, tiled=True)  7.07 us
    all_to_all x1, starting transfers between devices, exchange_in_order(): lax.all_to_all(blocks, axes[k], split_axis=k, concat_axis=k, tiled=True)  6.6 us
  transfers between devices with their start and end apart: 4, of which 4 were waited for; matrix products, arithmetic and copies ran while one was open for 5% of the time, Pallas kernels for 0%

commit v1 on v0

--- a/solution.py
+++ b/solution.py
@@ -101,7 +101,18 @@
         return (stream.astype(jnp.float32) + keep_mask[:, :, None] * update).astype(jnp.bfloat16)
 
     left_side, right_side, gate_value = project(pair, 0)
-    partial_rows = contract_rows(left_side, lax.all_gather(right_side, ROW, axis=1, tiled=True))
+    partial_rows = contract_rows(
+        left_side,
+        jnp.concatenate(
+            lax.all_to_all(
+                jnp.stack(lax.axis_size(ROW) * [right_side]),
+                axis_name=ROW,
+                split_axis=0,
+                concat_axis=0,
+            ),
+            axis=1,
+        ),
+    )
     mixed_sum = sum_at_owner(partial_rows, "col", 2)
     stream = finish(pair, mixed_sum, gate_value, 0)
     left_side, right_side, gate_value = project(stream, 1)

time: 329 us -> 673 us (2.05)
  waiting for transfers between devices: 197 us -> 508 us
  starting transfers between devices: 10.7 us -> 43.8 us
    all_to_all x0 -> x1, waiting for transfers between devices: none -> 402 us  [body(): lax.all_to_all(jnp.stack(lax.axis_size(ROW) * [right_side]), axis_name=RO...]
    all_gather x2 -> x1, waiting for transfers between devices: 104 us -> 14 us  [body(): lax.all_gather(right_side, ROW, axis=1, tiled=True)]
    all_to_all x0 -> x1, starting transfers between devices: none -> 25.5 us  [body(): lax.all_to_all(jnp.stack(lax.axis_size(ROW) * [right_side]), axis_name=RO...]
    all_gather x2 -> x1, local copies, waits for them, and re-layouts: 31.1 us -> 15.6 us  [body(): lax.all_gather(right_side, ROW, axis=1, tiled=True)]
    reshape x0 -> x1, local copies, waits for them, and re-layouts: none -> 14 us  [body(): jnp.concatenate(lax.all_to_all(jnp.stack(lax.axis_size(ROW) * [right_side...]
    all_to_all x1, starting transfers between devices: 6.6 us -> 13.8 us  [exchange_in_order(): lax.all_to_all(blocks, axes[k], split_axis=k, concat_axis=k, tiled=True)]
  transfers between devices with their start and end apart: 4 -> 4, of which waited for: 4 -> 4; matrix products, arithmetic and copies ran while one was open for 5% -> 2% of each run, Pallas kernels for 0% -> 0%
where the time goes in v1:
time: 673 us; the launch traced here: 672 us
  waiting for transfers between devices  508 us (75%)
  local copies, waits for them, and re-layouts  55.7 us (8%)
  starting transfers between devices  43.8 us (7%)
  blocking collectives  24.3 us (4%)
  matrix products  19 us (3%)
  between operations  14.4 us (2%)
    all_to_all x1, waiting for transfers between devices, body(): lax.all_to_all(jnp.stack(lax.axis_size(ROW) * [right_side]), axis_name=RO...  402 us
    all_to_all x1, waiting for transfers between devices, exchange_in_order(): lax.all_to_all(blocks, axes[k], split_axis=k, concat_axis=k, tiled=True)  66.2 us
    all_to_all x1, waiting for transfers between devices, sum_at_owner(): lax.all_to_all(blocks, axis, split_axis=0, concat_axis=0, tiled=True)  26.4 us
    all_to_all x1, starting transfers between devices, body(): lax.all_to_all(jnp.stack(lax.axis_size(ROW) * [right_side]), axis_name=RO...  25.5 us
    all_to_all x1, blocking collectives, sent_to_all(): return lax.all_to_all(copies, axis, split_axis=0, concat_axis=0, tiled=True)  17.4 us
    all_gather x1, local copies, waits for them, and re-layouts, body(): lax.all_gather(right_side, ROW, axis=1, tiled=True)  15.6 us
    reshape x1, local copies, waits for them, and re-layouts, body(): jnp.concatenate(lax.all_to_all(jnp.stack(lax.axis_size(ROW) * [right_side...  14 us
    all_gather x1, waiting for transfers between devices, body(): lax.all_gather(right_side, ROW, axis=1, tiled=True)  14 us
  transfers between devices with their start and end apart: 4, of which 4 were waited for; matrix products, arithmetic and copies ran while one was open for 2% of the time, Pallas kernels for 0%

profile of v1, /device:TPU:33, one launch (start us, length us, event | category | flops | bytes accessed | tf_op | source)
XLA Modules:
  0.0 671.9 jit_solution(17294297833036400189)
XLA Ops:
  7.2 1.1 convert_reduce_fusion
  8.4 1.4 fusion.20
  9.9 1.0 fusion.68
  11.1 1.5 convolution_bitcast_fusion.1
  12.8 5.8 stack.5
  18.6 25.5 %all-to-all-start = ((bf16[32,128,12,96]{1,3,2,0:T(8,128)(2,1)}), bf16[32,128,12,96]{1,3,2,0:T(8,128)(2,1)}, u32[]{:S(2)}, u32[]{:S(2)}) async-start(bf16[32,128,12,96]{1,3,2,0:T(8,128)(2,1)} %stack.5), calls=%async_computation | async-start | bytes 18874368 | tf_op jit(solution)/shard_map/all_to_all | solution.py:107
  44.3 1.2 copy.71
  45.5 401.8 %all-to-all-done = bf16[32,128,12,96]{1,3,2,0:T(8,128)(2,1)} async-done(((bf16[32,128,12,96]{1,3,2,0:T(8,128)(2,1)}), bf16[32,128,12,96]{1,3,2,0:T(8,128)(2,1)}, u32[]{:S(2)}, u32[]{:S(2)}) %all-to-all-start) | async-done | bytes 9437216 | tf_op jit(solution)/shard_map/all_to_all | solution.py:107
  447.3 14.0 %copy.72 = bf16[128,384,96]{1,2,0:T(8,128)(2,1)} copy(bf16[128,384,96]{0,2,1:T(8,128)(2,1)} %bitcast.14) | data formatting | bytes 18874368 | tf_op jit(solution)/shard_map/reshape | solution.py:106
  461.4 5.6 fusion.72
  467.0 2.1 copy.73
  469.1 3.3 copy.74
  472.3 4.5 all-to-all-start.1
  477.6 1.3 fusion.11
  478.9 26.4 %all-to-all-done.1 = f32[4,128,12,96]{1,3,2,0:T(8,128)S(1)} async-done(((f32[4,128,12,96]{1,3,2,0:T(8,128)}), f32[4,128,12,96]{1,3,2,0:T(8,128)S(1)}, u32[]{:S(2)}, u32[]{:S(2)}) %all-to-all-start.1) | async-done | bytes 2359328 | tf_op jit(solution)/shard_map/all_to_all | solution.py:19
  507.9 1.1 fusion.44
  509.2 17.4 %all_to_all.25 = bf16[4,128,12,96]{1,3,2,0:T(8,128)(2,1)S(1)} all-to-all(bf16[4,128,12,96]{1,3,2,0:T(8,128)(2,1)S(1)} %broadcast_in_dim.2), channel_id=1, replica_groups=mesh['grp'=2,'row_0'=16,'row_1'=2,'col'=4] {'col'}, dimensions={0} | all-to-all | bytes 2359296 | tf_op jit(solution)/shard_map/all_to_all | solution.py:25
  526.6 1.1 copy.80
  527.7 2.2 reshape_reshape.3
  530.4 6.9 %all_to_all.26 = bf16[16,2,128,12,12]{2,0,4,3,1:T(8,128)(2,1)S(1)} all-to-all(bf16[16,2,128,12,12]{2,0,4,3,1:T(8,128)(2,1)S(1)} %copy.81), channel_id=1, replica_groups=mesh['grp'=2,'row_0'=16,'row_1'=2,'col'=4] {'row_1'}, dimensions={1} | all-to-all | bytes 2359296 | tf_op jit(solution)/shard_map/all_to_all | solution.py:43
  537.3 2.2 copy.82
  539.5 13.8 %all-to-all-start.4 = ((bf16[16,2,128,12,12]{2,1,4,3,0:T(2,128)(2,1)}), bf16[16,2,128,12,12]{2,1,4,3,0:T(2,128)(2,1)S(1)}, u32[]{:S(2)}, u32[]{:S(2)}) async-start(bf16[16,2,128,12,12]{2,1,4,3,0:T(2,128)(2,1)} %copy.82), calls=%async_computation.4 | async-start | bytes 2359296 | tf_op jit(solution)/shard_map/all_to_all | solution.py:43
  553.9 66.2 %all-to-all-done.4 = bf16[16,2,128,12,12]{2,1,4,3,0:T(2,128)(2,1)S(1)} async-done(((bf16[16,2,128,12,12]{2,1,4,3,0:T(2,128)(2,1)}), bf16[16,2,128,12,12]{2,1,4,3,0:T(2,128)(2,1)S(1)}, u32[]{:S(2)}, u32[]{:S(2)}) %all-to-all-start.4) | async-done | bytes 1179680 | tf_op jit(solution)/shard_map/all_to_all | solution.py:43
  620.1 1.0 copy.83
  621.1 0.8 copy.84
  621.9 1.2 reshape.168
  623.1 2.2 copy.87
  625.3 14.0 %all-gather.2.cloned.1.call-done = bf16[128,384,96]{0,2,1:T(8,128)(2,1)} async-done(((bf16[128,12,96]{0,2,1:T(8,128)(2,1)}), bf16[128,384,96]{0,2,1:T(8,128)(2,1)}) %all-gather.2.cloned.1.call-update) | async-done | bytes 9437200 | tf_op jit(solution)/shard_map/all_gather | solution.py:121
  639.3 15.6 %copy.88 = bf16[128,384,96]{2,1,0:T(8,128)(2,1)} copy(bf16[128,384,96]{0,2,1:T(8,128)(2,1)} %all-gather.2.cloned.1.call-done) | data formatting | bytes 18874368 | tf_op jit(solution)/shard_map/all_gather | solution.py:121
  654.8 5.8 fusion.70
  662.7 0.8 fusion.46
  663.6 1.5 fusion.16
  (47 shorter events, 7.2 us)
Async XLA Ops:
  6.5 656.1 %copy-start = (bf16[128,1024]{1,0:T(8,128)(2,1)S(1)}, bf16[128,1024]{1,0:T(8,128)(2,1)}, u32[]{:S(2)}) copy-start(bf16[128,1024]{1,0:T(8,128)(2,1)} %param.12) | copy-start | bytes 786436
  9.9 3.0 copy-start.5
  18.6 428.7 %all-to-all-start = ((bf16[32,128,12,96]{1,3,2,0:T(8,128)(2,1)}), bf16[32,128,12,96]{1,3,2,0:T(8,128)(2,1)}, u32[]{:S(2)}, u32[]{:S(2)}) async-start(bf16[32,128,12,96]{1,3,2,0:T(8,128)(2,1)} %stack.5), calls=%async_computation | async-start | bytes 18874368 | tf_op jit(solution)/shard_map/all_to_all | solution.py:107
  472.3 5.2 copy-start.1
  472.3 33.0 %all-to-all-start.1 = ((f32[4,128,12,96]{1,3,2,0:T(8,128)}), f32[4,128,12,96]{1,3,2,0:T(8,128)S(1)}, u32[]{:S(2)}, u32[]{:S(2)}) async-start(f32[4,128,12,96]{1,3,2,0:T(8,128)} %copy.74), calls=%async_computation.1 | async-start | bytes 4718592 | tf_op jit(solution)/shard_map/all_to_all | solution.py:19
  476.8 162.5 %all-gather.2.cloned.1.call-start = ((), (), s32[]{:S(2)}) async-start(), calls=%async_computation.5 | async-start | bytes 9732096 | tf_op jit(solution)/shard_map/all_gather | solution.py:121
  505.3 0.8 copy-start.3
  505.6 1.8 copy-start.2
  537.3 16.1 %copy-start.7 = (bf16[2,128,128]{2,1,0:T(8,128)(2,1)S(1)}, bf16[2,128,128]{2,1,0:T(8,128)(2,1)}, u32[]{:S(2)}) copy-start(bf16[2,128,128]{2,1,0:T(8,128)(2,1)} %param.10) | copy-start | bytes 196612
  539.5 80.5 %all-to-all-start.4 = ((bf16[16,2,128,12,12]{2,1,4,3,0:T(2,128)(2,1)}), bf16[16,2,128,12,12]{2,1,4,3,0:T(2,128)(2,1)S(1)}, u32[]{:S(2)}, u32[]{:S(2)}) async-start(bf16[16,2,128,12,12]{2,1,4,3,0:T(2,128)(2,1)} %copy.82), calls=%async_computation.4 | async-start | bytes 2359296 | tf_op jit(solution)/shard_map/all_to_all | solution.py:43
  660.7 0.8 copy-start.4
  662.7 0.9 copy-start.6
Sparse Core Ops, SparseCore 0:
  509.2 130.0 all-gather.1
